TPU v7x, 32 devices: a whole 2x2x4 slice. The times are simulated.
32 devices in a mesh: ctx: 32 (over z, y, x, core), head: 1.
Axes of the slice: x: 2, y: 2, z: 4, core: 2. Of those that a mesh axis runs over, the one named last changes fastest.
Arguments:
- queries: bfloat16 [6144, 4096], P('ctx', 'head'), may hold values from -6 to 6
- keys: bfloat16 [6144, 1024], P('ctx', 'head'), may hold values from -6 to 6
- values: bfloat16 [6144, 1024], P('ctx', 'head'), may hold values from -6 to 6
- retrieval: int32 [32], replicated, may hold values 0 or 1
- spans: int32 [2, 32], replicated, may hold values from 64 to 4096, as said below
- out_weight: bfloat16 [4096, 4096], P(None, 'head'), may hold values from -0.09375 to 0.09375
Outputs:
- layer_out: bfloat16 [6144, 4096], P('ctx', 'head')
Inputs may be any that keep to these rules, and one draw needn't show every extreme that they name: `spans`: row 0 lies within 64 to 128, row 1 within 2048 to 4096; some head has exactly 128 sink tokens and some head exactly 4096 recent tokens.
All inputs are finite; a program needn't handle non-finite values.
Results may differ from a plain program's by a relative error of at most 0.0075.
Values may be sent and summed in bfloat16 or wider, within the bound.
A program may use at most 192 MiB of HBM per device.

v0:
```python
import functools

import jax
import jax.numpy as jnp
from jax import lax
from jax.experimental import pallas as pl
from jax.experimental.pallas import tpu as pltpu
from jax.sharding import PartitionSpec as P

HD = 128
LOG2E = 1.4426950408889634
MASKED = -1e30
FLOOR = -1e29
FAR = 1 << 29


def attend_kernel(group, block, first_head, meta_ref, pos_ref, q_ref, k_ref, v_ref, o_ref, stacked, peak, total, accum):
    rows = q_ref.shape[0]
    scale = (HD ** -0.5) * LOG2E
    head = first_head + pl.program_id(0) * group
    first_row = pos_ref[0]
    last_row = first_row + rows - 1
    sinks = [meta_ref[0, head + r] for r in range(group)]
    windows = [meta_ref[1, head + r] for r in range(group)]
    widest = functools.reduce(jnp.maximum, windows)
    narrowest = functools.reduce(jnp.minimum, windows)
    most_sink = functools.reduce(jnp.maximum, sinks)

    for r in range(group):
        stacked[r * rows:(r + 1) * rows, :] = q_ref[:, r * HD:(r + 1) * HD]
    peak[...] = jnp.full_like(peak, FLOOR)
    total[...] = jnp.zeros_like(total)
    accum[...] = jnp.zeros_like(accum)

    def step(index, masked):
        start = pl.multiple_of(index * block, block)
        scores = lax.dot_general(
            stacked[...], k_ref[pl.ds(start, block), :], (((1,), (1,)), ((), ())),
            preferred_element_type=jnp.float32,
        )
        if masked:
            key_pos = start + lax.broadcasted_iota(jnp.int32, (rows, block), 1)
            gap = first_row - key_pos + lax.broadcasted_iota(jnp.int32, (rows, block), 0)
            parts = []
            for r in range(group):
                allowed = (gap >= 0) & ((gap < windows[r]) | (key_pos < sinks[r]))
                parts.append(jnp.where(allowed, scores[r * rows:(r + 1) * rows], MASKED))
            scores = jnp.concatenate(parts, axis=0)
        held = peak[...]
        fresh = jnp.maximum(held, jnp.max(scores, axis=-1, keepdims=True))
        peak[...] = fresh
        shrink = jnp.exp2((held - fresh) * scale)
        weights = jnp.exp2((scores - jnp.tile(fresh, (1, block // HD))) * scale)
        added = weights[:, :HD]
        for c in range(1, block // HD):
            added = added + weights[:, c * HD:(c + 1) * HD]
        total[...] = total[...] * shrink + added
        accum[...] = accum[...] * shrink + jnp.dot(
            weights.astype(jnp.bfloat16), v_ref[pl.ds(start, block), :],
            preferred_element_type=jnp.float32,
        )

    low = jnp.maximum(first_row - widest + 1, 0) // block
    high = last_row // block + 1
    full_low = jnp.minimum((jnp.maximum(last_row - narrowest + 1, 0) + block - 1) // block, high)
    full_high = jnp.maximum((first_row + 1) // block, full_low)
    sink_blocks = jnp.minimum((most_sink + block - 1) // block, low)
    count_low = jnp.maximum(full_low - low, 0)
    masked_count = sink_blocks + count_low + (high - full_high)

    def masked_step(i, carry):
        near = i - sink_blocks
        index = jnp.where(
            near < 0, i, jnp.where(near < count_low, low + near, full_high + near - count_low)
        )
        step(index, True)
        return carry

    def full_step(i, carry):
        step(i, False)
        return carry

    lax.fori_loop(0, masked_count, masked_step, 0)
    lax.fori_loop(full_low, full_high, full_step, 0)
    mixed = accum[...] / jnp.sum(total[...], axis=-1, keepdims=True)
    for r in range(group):
        o_ref[:, r * HD:(r + 1) * HD] = mixed[r * rows:(r + 1) * rows].astype(jnp.bfloat16)


def attend(queries, gathered, meta, position, group, first_kv, kv_count):
    rows = queries.shape[0]
    seq = gathered.shape[0]
    block = 512 if seq % 512 == 0 else HD
    smem = pl.BlockSpec(memory_space=pltpu.SMEM)
    return pl.pallas_call(
        functools.partial(attend_kernel, group, block, first_kv * group),
        grid=(kv_count,),
        out_shape=jax.ShapeDtypeStruct((rows, kv_count * group * HD), jnp.bfloat16),
        in_specs=[
            smem,
            smem,
            pl.BlockSpec((rows, group * HD), lambda g: (0, first_kv + g)),
            pl.BlockSpec((seq, HD), lambda g: (0, g)),
            pl.BlockSpec((seq, HD), lambda g: (0, kv_count + g)),
        ],
        out_specs=pl.BlockSpec((rows, group * HD), lambda g: (0, g)),
        scratch_shapes=[
            pltpu.VMEM((group * rows, HD), jnp.bfloat16),
            pltpu.VMEM((group * rows, HD), jnp.float32),
            pltpu.VMEM((group * rows, HD), jnp.float32),
            pltpu.VMEM((group * rows, HD), jnp.float32),
        ],
        compiler_params=pltpu.CompilerParams(dimension_semantics=("arbitrary",)),
        cost_estimate=pl.CostEstimate(
            flops=8 * kv_count * group * rows * seq * HD,
            bytes_accessed=2 * kv_count * seq * HD * 2,
            transcendentals=kv_count * group * rows * seq,
        ),
    )(meta, position, queries, gathered, gathered)


def body(queries, keys, values, retrieval, spans, out_weight):
    rows = queries.shape[0]
    local_heads = queries.shape[1] // HD
    kv_heads = keys.shape[1] // HD
    group = local_heads // kv_heads
    head_first = lax.axis_index("head") * local_heads
    windows = jnp.where(retrieval > 0, FAR, spans[1])
    meta = lax.dynamic_slice_in_dim(jnp.stack([spans[0], windows]), head_first, local_heads, axis=1)
    position = (lax.axis_index("ctx") * rows).reshape(1).astype(jnp.int32)
    early = max(1, kv_heads * 3 // 4)
    spans_of = [(0, early)] + ([(early, kv_heads - early)] if early < kv_heads else [])
    gathered = []
    for g, count in spans_of:
        columns = slice(g * HD, (g + count) * HD)
        own = jnp.concatenate([keys[:, columns], values[:, columns]], axis=1)
        gathered.append(lax.all_gather(own, "ctx", axis=0, tiled=True))
    pieces = [
        attend(queries, held, meta, position, group, g, count)
        for held, (g, count) in zip(gathered, spans_of)
    ]
    attended = jnp.concatenate(pieces, axis=1)
    features = lax.all_gather(attended, "head", axis=1, tiled=True)
    projected = jnp.dot(features, out_weight, preferred_element_type=jnp.float32)
    return projected.astype(jnp.bfloat16)


def solution(mesh):
    in_specs = (P("ctx", "head"), P("ctx", "head"), P("ctx", "head"), P(), P(), P(None, "head"))
    out_specs = P("ctx", "head")
    return jax.shard_map(body, mesh=mesh, in_specs=in_specs, out_specs=out_specs, check_vma=False)
```

profile of v0, /device:TPU:29, one launch (start us, length us, event | category | flops | bytes accessed | tf_op | source)
XLA Modules:
  0.0 288.3 jit_solution(15865932221515424592)
XLA Ops:
  6.5 0.0 slice-start
  6.5 0.0 slice-start.1
  6.5 0.0 all-gather.5.cloned.1.call-start
  6.5 1.0 slice.22
  7.5 0.9 slice.23
  8.4 0.7 pad_maximum_fusion.1
  9.1 0.0 copy-start
  9.1 0.0 copy-start.1
  9.1 0.0 slice-start.2
  9.1 0.0 all-gather.5.cloned.1.call-update
  9.1 0.0 all-gather.3.cloned.1.call-start
  9.2 0.0 slice-done
  9.2 0.0 slice-done.1
  9.2 0.9 pad_maximum_fusion
  10.1 0.0 all-gather.3.cloned.1.call-update
  10.1 0.0 copy-done
  10.1 0.0 copy-done.1
  10.1 0.0 slice-done.2
  10.1 0.5 pad_add_fusion.meta_ref
  10.7 68.6 %all-gather.5.cloned.1.call-done.k_ref.v_ref = bf16[6144,512]{1,0:T(8,128)(2,1)} async-done(((bf16[192,512]{1,0:T(8,128)(2,1)}), bf16[6144,512]{1,0:T(8,128)(2,1)}) %all-gather.5.cloned.1.call-update) | async-done | bytes 6291472 | tf_op jit(solution)/shard_map/all_gather | solution.py:137
  79.3 23.5 %shard_map.65 = bf16[192,1024]{1,0:T(8,128)(2,1)} custom-call(s32[2,32]{1,0:T(2,128)} %pad_add_fusion.meta_ref, s32[1]{0:T(128)} %bitcast.2.pos_ref, bf16[192,4096]{1,0:T(8,128)(2,1)} %q_ref.3, bf16[6144,512]{1,0:T(8,128)(2,1)} %all-gather.5.cloned.1.call-done.k_ref.v_ref, bf16[6144,512]{1,0:T(8,128)(2,1)} %all-gather.5.cloned.1.call-done.k_ref.v_ref), custom_call_target="tpu_custom_call" | custom-call | flops 9663676416 | bytes 6291456 | tf_op jit(solution)/shard_map/pallas_call | solution.py:95
  102.8 0.0 copy-start.2
  102.8 101.6 %all-gather.3.cloned.1.call-done.k_ref.v_ref = bf16[6144,1536]{1,0:T(8,128)(2,1)} async-done(((bf16[192,1536]{1,0:T(8,128)(2,1)}), bf16[6144,1536]{1,0:T(8,128)(2,1)}) %all-gather.3.cloned.1.call-update) | async-done | bytes 18874384 | tf_op jit(solution)/shard_map/all_gather | solution.py:137
  204.4 61.6 %shard_map.64 = bf16[192,3072]{1,0:T(8,128)(2,1)} custom-call(s32[2,32]{1,0:T(2,128)} %pad_add_fusion.meta_ref, s32[1]{0:T(128)} %bitcast.2.pos_ref, bf16[192,4096]{1,0:T(8,128)(2,1)} %q_ref.3, bf16[6144,1536]{1,0:T(8,128)(2,1)} %all-gather.3.cloned.1.call-done.k_ref.v_ref, bf16[6144,1536]{1,0:T(8,128)(2,1)} %all-gather.3.cloned.1.call-done.k_ref.v_ref), custom_call_target="tpu_custom_call" | custom-call | flops 28991029248 | bytes 18874368 | tf_op jit(solution)/shard_map/pallas_call | solution.py:95
  266.0 0.0 copy-done.2
  266.0 15.5 %convolution_convert_fusion = bf16[192,4096]{1,0:T(8,128)(2,1)} fusion(bf16[4096,4096]{1,0:T(8,128)(2,1)} %param.11, bf16[192,1024]{1,0:T(8,128)(2,1)S(1)} %copy-done.2, bf16[192,3072]{1,0:T(8,128)(2,1)} %shard_map.64), kind=kOutput, calls=%fused_computation | convolution fusion | flops 6446383104 | bytes 36700160 | tf_op jit(solution)/shard_map/dot_general | solution.py:144
  (1 shorter events, 0.0 us)
Async XLA Ops:
  6.5 2.7 slice-start
  6.5 2.7 slice-start.1
  6.5 72.7 %all-gather.5.cloned.1.call-start = ((), (), s32[]{:S(2)}) async-start(), calls=%async_computation.1 | async-start | bytes 6488064 | tf_op jit(solution)/shard_map/all_gather | solution.py:137
  9.1 1.0 copy-start
  9.1 1.0 copy-start.1
  9.1 1.0 slice-start.2
  9.1 195.2 %all-gather.3.cloned.1.call-start = ((), (), s32[]{:S(2)}) async-start(), calls=%async_computation | async-start | bytes 19464192 | tf_op jit(solution)/shard_map/all_gather | solution.py:137
  102.8 163.3 %copy-start.2 = (bf16[192,1024]{1,0:T(8,128)(2,1)S(1)}, bf16[192,1024]{1,0:T(8,128)(2,1)}, u32[]{:S(2)}) copy-start(bf16[192,1024]{1,0:T(8,128)(2,1)} %shard_map.65) | copy-start | bytes 1179652
Sparse Core Ops, SparseCore 0:
  10.2 69.0 all-gather.4
  82.2 122.1 all-gather.2
where the time goes:
time: 290 us; the launch traced here: 288 us
  waiting for transfers between devices  170 us (59%)
  Pallas kernels  85.1 us (29%)
  matrix products  15.5 us (5%)
  between operations  13.5 us (5%)
    all_gather x2, waiting for transfers between devices, body(): gathered.append(lax.all_gather(own, 'ctx', axis=0, tiled=True))  170 us
    pallas_call x2, Pallas kernels, attend(): pl.pallas_call(functools.partial(attend_kernel, group, block, first_kv *...  85.1 us
    dot_general x1, matrix products, body(): jnp.dot(features, out_weight, preferred_element_type=jnp.float32)  15.5 us
  transfers between devices with their start and end apart: 2, of which 2 were waited for; matrix products, arithmetic and copies ran while one was open for 0% of the time, Pallas kernels for 8%

commit v1 on v0

v1 whole, which is shorter than its diff:
```python
import functools

import jax
import jax.numpy as jnp
from jax import lax
from jax.experimental import pallas as pl
from jax.experimental.pallas import tpu as pltpu
from jax.sharding import PartitionSpec as P

HD = 128
LOG2E = 1.4426950408889634
MASKED = -1e30
FLOOR = -1e29
FAR = 1 << 29
LEAST_RECENT = 2048
MOST_SINK = 128
W_SLOTS = 4
MESH = pl.DeviceIdType.MESH


def across(a, b, size):
    if size & (size - 1):
        return (a + b) % size
    total = 0
    bit = 1
    while bit < size:
        x, y = (a // bit) % 2, (b // bit) % 2
        total = total + bit * (x + y - 2 * x * y)
        bit *= 2
    return total


def back(a, b, size):
    if size & (size - 1):
        return (a + size - b) % size
    return across(a, b, size)


def layer_kernel(
    planes, members, rows, group, fused,
    q_hbm, k_hbm, v_hbm, retrieval_ref, spans_ref, *rest,
):
    if fused:
        w_hbm, out_ref, *rest = rest
    else:
        out_ref, *rest = rest
    (q_all, keys, values, peak, total, accum, done, feats, kv_in, kv_out, q_in, q_out, near_out, o_in, o_out, *rest) = rest
    block = members * rows
    width = group * HD
    scale = (HD ** -0.5) * LOG2E
    me = lax.axis_index("ctx")
    plane, member = me // members, me % members
    first_head = lax.axis_index("head") * (members * group) + member * group
    sinks = [spans_ref[0, first_head + h] for h in range(group)]
    windows = [
        jnp.where(retrieval_ref[first_head + h] > 0, FAR, spans_ref[1, first_head + h]) for h in range(group)
    ]
    has_below, has_above = plane > 0, plane < planes - 1

    def lanes(index, count):
        return pl.ds(pl.multiple_of(index * count, count), count)

    def span_of(index, count):
        return pl.ds(pl.multiple_of(index * count, rows), count)

    if fused:
        w_buf, product, w_sem = rest

        def load_w(step):
            owner = back(member, members - 1 - step, members)
            return pltpu.make_async_copy(
                w_hbm.at[lanes(owner, width), :], w_buf.at[step % W_SLOTS], w_sem.at[step % W_SLOTS]
            )

    own_rows = span_of(me, rows)

    def own_kv(c):
        source, target = ((k_hbm, keys), (v_hbm, values))[c]
        return pltpu.make_async_copy(
            source.at[:, lanes(member, HD)], target.at[own_rows, :], kv_in.at[0, member, c]
        )

    def own_q(h):
        return pltpu.make_async_copy(
            q_hbm.at[:, lanes(member * group + h, HD)],
            q_all.at[span_of(member * group + h, rows), :],
            q_in.at[member, h],
        )

    def near_kv(peer, c):
        source, target = ((k_hbm, keys), (v_hbm, values))[c]
        return pltpu.make_async_remote_copy(
            src_ref=source.at[:, lanes(peer, HD)],
            dst_ref=target.at[own_rows, :],
            send_sem=near_out.at[peer, c],
            recv_sem=kv_in.at[0, member, c],
            device_id={"ctx": plane * members + peer},
            device_id_type=MESH,
        )

    def near_q(peer, h):
        return pltpu.make_async_remote_copy(
            src_ref=q_hbm.at[:, lanes(peer * group + h, HD)],
            dst_ref=q_all.at[span_of(member * group + h, rows), :],
            send_sem=q_out.at[peer, h],
            recv_sem=q_in.at[member, h],
            device_id={"ctx": plane * members + peer},
            device_id_type=MESH,
        )

    def up_kv(step, peer, c):
        target = (keys, values)[c]
        piece = span_of((plane - step) * members + peer, rows)
        return pltpu.make_async_remote_copy(
            src_ref=target.at[piece, :],
            dst_ref=target.at[piece, :],
            send_sem=kv_out.at[step, peer, c],
            recv_sem=kv_in.at[step + 1, peer, c],
            device_id={"ctx": me + members},
            device_id_type=MESH,
        )

    def landed_kv(step, peer, c):
        target = (keys, values)[c]
        piece = target.at[span_of((plane - step) * members + peer, rows), :]
        return pltpu.make_async_copy(piece, piece, kv_in.at[step, peer, c])

    def give_o(peer):
        return pltpu.make_async_remote_copy(
            src_ref=done.at[span_of(peer, rows), :],
            dst_ref=feats.at[:, lanes(member, width)],
            send_sem=o_out.at[peer],
            recv_sem=o_in.at[member],
            device_id={"ctx": plane * members + peer},
            device_id_type=MESH,
        )

    def keep_o():
        return pltpu.make_async_copy(
            done.at[span_of(member, rows), :], feats.at[:, lanes(member, width)], o_in.at[member]
        )

    for c in range(2):
        own_kv(c).start()
    for h in range(group):
        own_q(h).start()
    if fused:
        for step in range(min(W_SLOTS, members)):
            load_w(step).start()

    barrier = pltpu.get_barrier_semaphore()
    for offset in range(1, members):
        peer = across(member, offset, members)
        pl.semaphore_signal(barrier, inc=1, device_id={"ctx": plane * members + peer}, device_id_type=MESH)

    @pl.when(has_below)
    def _():
        pl.semaphore_signal(barrier, inc=1, device_id={"ctx": me - members}, device_id_type=MESH)

    @pl.when(has_above)
    def _():
        pl.semaphore_signal(barrier, inc=1, device_id={"ctx": me + members}, device_id_type=MESH)

    pl.semaphore_wait(barrier, members - 1 + has_below.astype(jnp.int32) + has_above.astype(jnp.int32))

    for offset in range(members - 1, 0, -1):
        peer = across(member, offset, members)
        for c in range(2):
            near_kv(peer, c).start()
    for offset in range(members - 1, 0, -1):
        peer = across(member, offset, members)
        for h in range(group):
            near_q(peer, h).start()

    peak[...] = jnp.full_like(peak, FLOOR)
    total[...] = jnp.zeros_like(total)
    accum[...] = jnp.zeros_like(accum)

    def take_kv(step):
        def one(order, carry):
            peer = back(member, order, members)
            for c in range(2):
                landed_kv(step, peer, c).wait()

            @pl.when(has_above)
            def _():
                for c in range(2):
                    up_kv(step, peer, c).start()

            return carry

        lax.fori_loop(0, members, one, 0)

    def tile(index, start, count, allow):
        key_rows = pl.ds(start, count)

        def head_rows(h):
            return span_of(index * group + h, rows)

        def score(h):
            return lax.dot_general(
                q_all[head_rows(h), :], keys[key_rows, :], (((1,), (1,)), ((), ())),
                preferred_element_type=jnp.float32,
            )

        pending = score(0)
        for h in range(group):
            following = score(h + 1) if h + 1 < group else None
            at = head_rows(h)
            scores = allow(h, pending)
            held = peak[at, :]
            fresh = jnp.maximum(held, jnp.max(scores, axis=-1, keepdims=True))
            peak[at, :] = fresh
            shrink = jnp.exp2((held - fresh) * scale)
            weights = jnp.exp2((scores - jnp.tile(fresh, (1, count // HD))) * scale)
            added = weights[:, :HD]
            for c in range(1, count // HD):
                added = added + weights[:, c * HD:(c + 1) * HD]
            total[at, :] = total[at, :] * shrink + added
            accum[at, :] = accum[at, :] * shrink + jnp.dot(
                weights.astype(jnp.bfloat16), values[key_rows, :], preferred_element_type=jnp.float32
            )
            pending = following

    def gaps(count):
        return lax.broadcasted_iota(jnp.int32, (rows, count), 0) - lax.broadcasted_iota(
            jnp.int32, (rows, count), 1
        )

    def finish(index):
        for h in range(group):
            at = span_of(index * group + h, rows)
            mixed = accum[at, :] / jnp.sum(total[at, :], axis=-1, keepdims=True)
            done[span_of(index, rows), h * HD:(h + 1) * HD] = mixed.astype(jnp.bfloat16)

        @pl.when(index == member)
        def _():
            keep_o().start()

        @pl.when(index != member)
        def _():
            give_o(index).start()

    def own_tile(count):
        def run(index, carry):
            for h in range(group):
                piece = q_all.at[span_of(index * group + h, rows), :]
                pltpu.make_async_copy(piece, piece, q_in.at[index, h]).wait()

            def allow(h, scores):
                return jnp.where(gaps(count) >= -index * rows, scores, MASKED)

            tile(index, pl.multiple_of(plane * block, block), count, allow)

            @pl.when(plane == 0)
            def _():
                finish(index)

            return carry

        return run

    take_kv(0)
    half = members // 2
    if half and half * rows % HD == 0:
        lax.fori_loop(0, half, own_tile(half * rows), 0)
        lax.fori_loop(half, members, own_tile(block), 0)
    else:
        lax.fori_loop(0, members, own_tile(block), 0)

    def far_block(step, carry):
        take_kv(step)
        start = pl.multiple_of((plane - step) * block, block)

        def far_tile(order, inner):
            index = across(member, members - 1 - order, members)

            def allow(h, scores):
                gap = gaps(block)
                near = gap < windows[h] - (step * block + index * rows)
                column = lax.broadcasted_iota(jnp.int32, (rows, MOST_SINK), 1)
                sunk = near[:, :MOST_SINK] | (column < sinks[h] - (plane - step) * block)
                near = jnp.concatenate([sunk, near[:, MOST_SINK:]], axis=1)
                return jnp.where(near, scores, MASKED)

            tile(index, start, block, allow)

            @pl.when(step == plane)
            def _():
                finish(index)

            return inner

        lax.fori_loop(0, members, far_tile, 0)
        return carry

    lax.fori_loop(1, plane + 1, far_block, 0)

    if fused:
        columns = w_buf.shape[2]
        chunk = 512 if columns % 512 == 0 else columns
        product[...] = jnp.zeros_like(product)

        def project(step, carry):
            owner = back(member, members - 1 - step, members)
            piece = feats.at[:, lanes(owner, width)]
            pltpu.make_async_copy(piece, piece, o_in.at[owner]).wait()
            load_w(step).wait()
            slot = step % W_SLOTS
            features = feats[:, lanes(owner, width)]

            def part(c, inner):
                at = lanes(c, chunk)
                product[:, at] = product[:, at] + jnp.dot(
                    features, w_buf[slot, :, at], preferred_element_type=jnp.float32
                )
                return inner

            lax.fori_loop(0, columns // chunk, part, 0)

            @pl.when(step + W_SLOTS < members)
            def _():
                load_w(step + W_SLOTS).start()

            return carry

        lax.fori_loop(0, members, project, 0)
        out_ref[...] = product[...].astype(out_ref.dtype)
    else:
        for source in range(members):
            piece = feats.at[:, source * width:(source + 1) * width]
            pltpu.make_async_copy(piece, piece, o_in.at[source]).wait()
        out_ref[...] = feats[...]

    for offset in range(1, members):
        peer = across(member, offset, members)
        for c in range(2):
            near_kv(peer, c).wait_send()
        for h in range(group):
            near_q(peer, h).wait_send()
        give_o(peer).wait_send()

    @pl.when(has_above)
    def _():
        def sent(step, carry):
            def one(peer, inner):
                for c in range(2):
                    up_kv(step, peer, c).wait_send()
                return inner

            return lax.fori_loop(0, members, one, carry)

        lax.fori_loop(0, plane + 1, sent, 0)


def body(planes, members, fused, queries, keys, values, retrieval, spans, out_weight):
    rows = queries.shape[0]
    group = queries.shape[1] // keys.shape[1]
    width = group * HD
    block = members * rows
    if block > LEAST_RECENT or block % HD or block < MOST_SINK:
        raise ValueError("block size")
    anywhere = pl.BlockSpec(memory_space=pl.ANY)
    smem = pl.BlockSpec(memory_space=pltpu.SMEM)
    stacked = group * block
    scratch = [
        pltpu.VMEM((stacked, HD), jnp.bfloat16),
        pltpu.VMEM((planes * block, HD), jnp.bfloat16),
        pltpu.VMEM((planes * block, HD), jnp.bfloat16),
        pltpu.VMEM((stacked, HD), jnp.float32),
        pltpu.VMEM((stacked, HD), jnp.float32),
        pltpu.VMEM((stacked, HD), jnp.float32),
        pltpu.VMEM((block, width), jnp.bfloat16),
        pltpu.VMEM((rows, members * width), jnp.bfloat16),
        pltpu.SemaphoreType.DMA((planes, members, 2)),
        pltpu.SemaphoreType.DMA((planes, members, 2)),
        pltpu.SemaphoreType.DMA((members, group)),
        pltpu.SemaphoreType.DMA((members, group)),
        pltpu.SemaphoreType.DMA((members, 2)),
        pltpu.SemaphoreType.DMA((members,)),
        pltpu.SemaphoreType.DMA((members,)),
    ]
    operands = [queries, keys, values, retrieval, spans]
    in_specs = [anywhere, anywhere, anywhere, smem, smem]
    columns = members * width
    if fused:
        columns = out_weight.shape[1]
        operands.append(out_weight)
        in_specs.append(anywhere)
        scratch += [
            pltpu.VMEM((min(W_SLOTS, members), width, columns), jnp.bfloat16),
            pltpu.VMEM((rows, columns), jnp.float32),
            pltpu.SemaphoreType.DMA((min(W_SLOTS, members),)),
        ]
    result = pl.pallas_call(
        functools.partial(layer_kernel, planes, members, rows, group, fused),
        out_shape=jax.ShapeDtypeStruct((rows, columns), jnp.bfloat16),
        in_specs=in_specs,
        out_specs=pl.BlockSpec(memory_space=pltpu.VMEM),
        scratch_shapes=scratch,
        compiler_params=pltpu.CompilerParams(
            collective_id=0, has_side_effects=True, vmem_limit_bytes=60 * 2 ** 20
        ),
    )(*operands)
    if fused:
        return result
    features = lax.all_gather(result, "head", axis=1, tiled=True)
    return jnp.dot(features, out_weight, preferred_element_type=jnp.float32).astype(jnp.bfloat16)


def solution(mesh):
    ctx, heads = mesh.shape["ctx"], mesh.shape["head"]

    def step(queries, keys, values, retrieval, spans, out_weight):
        members = keys.shape[1] // HD
        if ctx % members:
            raise ValueError("members")
        return body(ctx // members, members, heads == 1, queries, keys, values, retrieval, spans, out_weight)

    in_specs = (P("ctx", "head"), P("ctx", "head"), P("ctx", "head"), P(), P(), P(None, "head"))
    return jax.shard_map(step, mesh=mesh, in_specs=in_specs, out_specs=P("ctx", "head"), check_vma=False)
```

time: 290 us -> 118 us (0.41)
  waiting for transfers between devices: 170 us -> 0 us
  Pallas kernels: 85.1 us -> 114 us
  matrix products: 15.5 us -> 0 us
  between operations: 13.5 us -> 0.01 us
    all_gather x2 -> x0, waiting for transfers between devices: 170 us -> none  [body(): gathered.append(lax.all_gather(own, 'ctx', axis=0, tiled=True))]
    pallas_call x2 -> x1, Pallas kernels: 85.1 us -> 114 us  [body(): pl.pallas_call(functools.partial(layer_kernel, planes, members, rows, gro...]
    dot_general x1 -> x0, matrix products: 15.5 us -> none  [body(): jnp.dot(features, out_weight, preferred_element_type=jnp.float32)]
  transfers between devices with their start and end apart: 2 -> 0, of which waited for: 2 -> 0; matrix products, arithmetic and copies ran while one was open for 0% -> 0% of each run, Pallas kernels for 8% -> 0%
where the time goes in v1:
time: 118 us; the launch traced here: 117 us
  Pallas kernels  114 us (97%)
  local copies, waits for them, and re-layouts  2.7 us (2%)
    pallas_call x1, Pallas kernels, body(): pl.pallas_call(functools.partial(layer_kernel, planes, members, rows, gro...  114 us
    unnamed x1, local copies, waits for them, and re-layouts  2.7 us

profile of v1, /device:TPU:29, one launch (start us, length us, event | category | flops | bytes accessed | tf_op | source)
XLA Modules:
  0.0 116.9 jit_solution(2495419193386690028)
XLA Ops:
  0.0 114.1 %shard_map.64 = bf16[192,4096]{1,0:T(8,128)(2,1)} custom-call(bf16[192,4096]{1,0:T(8,128)(2,1)} %q_hbm.1, bf16[192,1024]{1,0:T(8,128)(2,1)} %k_hbm.1, bf16[192,1024]{1,0:T(8,128)(2,1)} %v_hbm.1, s32[32]{0:T(128)} %retrieval_ref.1, s32[2,32]{1,0:T(2,128)} %spans_ref.1, bf16[4096,4096]{1,0:T(8,128)(2,1)} %rest_0_.1), custom_call_target="tpu_custom_call" | custom-call | tf_op jit(solution)/shard_map/pallas_call | solution.py:395
  114.2 2.7 %copy.8 = bf16[192,4096]{1,0:T(8,128)(2,1)} copy(bf16[192,4096]{1,0:T(8,128)(2,1)} %shard_map.64) | data formatting | bytes 3145728

commit v2 on v1

v2 whole, which is shorter than its diff:
```python
import functools

import jax
import jax.numpy as jnp
from jax import lax
from jax.experimental import pallas as pl
from jax.experimental.pallas import tpu as pltpu
from jax.sharding import PartitionSpec as P

HD = 128
LOG2E = 1.4426950408889634
MASKED = -1e30
FLOOR = -1e29
FAR = 1 << 29
LEAST_RECENT = 2048
MOST_SINK = 128
W_SLOTS = 4
W_COLUMNS = 1024
CORES = 2
MESH = pl.DeviceIdType.MESH


def across(a, b, size):
    if size & (size - 1):
        return (a + b) % size
    total = 0
    bit = 1
    while bit < size:
        x, y = (a // bit) % 2, (b // bit) % 2
        total = total + bit * (x + y - 2 * x * y)
        bit *= 2
    return total


def back(a, b, size):
    if size & (size - 1):
        return (a + size - b) % size
    return across(a, b, size)


def layer_kernel(
    planes, members, rows, group, fused,
    q_hbm, k_hbm, v_hbm, retrieval_ref, spans_ref, *rest,
):
    if fused:
        w_hbm, out_ref, *rest = rest
    else:
        out_ref, *rest = rest
    (q_all, kv, peak, total, accum, done, feats, gap_ref, near_in, near_out, kv_in, up_out, side_out,
     q_in, q_out, o_in, o_out, *rest) = rest
    chips, half = members // CORES, group // CORES
    block, tall, width = members * rows, half * rows, half * HD
    scale = (HD ** -0.5) * LOG2E
    me = lax.axis_index("ctx")
    plane, member = me // members, me % members
    chip, core = member // CORES, member % CORES
    partner = chip * CORES + (1 - core)
    has_below, has_above = plane > 0, plane < planes - 1
    head_base = lax.axis_index("head") * (members * group)

    def head_of(at_chip, at_core, g):
        return (at_chip * CORES + g) * group + at_core * half

    sinks, windows = [], []
    for g in range(CORES):
        for h in range(half):
            head = head_base + head_of(chip, core, g) + h
            sinks.append(spans_ref[0, head])
            windows.append(jnp.where(retrieval_ref[head] > 0, FAR, spans_ref[1, head]))

    def lanes(start, count):
        return pl.ds(pl.multiple_of(start * HD, HD), count * HD)

    def span_of(index, count):
        return pl.ds(pl.multiple_of(index * rows, rows), count * rows)

    def peer_id(peer):
        return {"ctx": plane * members + peer}

    def remote(source, target, send_sem, recv_sem, device_id):
        return pltpu.make_async_remote_copy(
            src_ref=source, dst_ref=target, send_sem=send_sem, recv_sem=recv_sem,
            device_id=device_id, device_id_type=MESH,
        )

    def kv_piece(g, at_plane, source):
        return kv.at[span_of((g * planes + at_plane) * members + source, 1), :]

    def near_kv(to_chip, g, c):
        source = (k_hbm, v_hbm)[c].at[:, lanes(to_chip * CORES + g, 1)]
        target = kv.at[span_of((g * planes + plane) * members + member, 1), c * HD:(c + 1) * HD]
        return source, target

    def own_kv(g, c):
        return pltpu.make_async_copy(*near_kv(chip, g, c), near_in.at[g, chip, c])

    def give_kv(to_chip, g, c):
        return remote(
            *near_kv(to_chip, g, c), near_out.at[to_chip, g, c], near_in.at[g, chip, c],
            peer_id(to_chip * CORES + core),
        )

    def up_kv(g, step, at_chip):
        piece = kv_piece(g, plane - step, at_chip * CORES + core)
        return remote(
            piece, piece, up_out.at[step, g, at_chip], kv_in.at[step + 1, g, at_chip, 0], {"ctx": me + members}
        )

    def side_kv(g, step, at_chip):
        piece = kv_piece(g, plane - step, at_chip * CORES + core)
        return remote(
            piece, piece, side_out.at[step, g, at_chip], kv_in.at[step, g, at_chip, 1], peer_id(partner)
        )

    def q_piece(peer, head):
        at_chip, at_core = peer // CORES, peer % CORES
        source = q_hbm.at[:, lanes(head_of(at_chip, at_core, head // half) + head % half, 1)]
        return source, q_all.at[span_of(member * group + head, 1), :]

    def own_q(head):
        return pltpu.make_async_copy(*q_piece(member, head), q_in.at[member, head])

    def give_q(peer, head):
        return remote(*q_piece(peer, head), q_out.at[peer, head], q_in.at[member, head], peer_id(peer))

    def o_piece(g, peer):
        return (
            done.at[span_of(peer, 1), g * width:(g + 1) * width],
            feats.at[:, lanes(head_of(chip, core, g), half)],
        )

    def keep_o(g):
        return pltpu.make_async_copy(*o_piece(g, member), o_in.at[member, g])

    def give_o(g, peer):
        return remote(*o_piece(g, peer), o_out.at[peer, g], o_in.at[member, g], peer_id(peer))

    def landed(piece, sem):
        pltpu.make_async_copy(piece, piece, sem).wait()

    if fused:
        w_buf, product, w_sem = rest
        slots = w_buf.shape[0]

        def load_w(step):
            g, order = step // chips, step % chips
            owner = back(chip, chips - 1 - order, chips)
            return pltpu.make_async_copy(
                w_hbm.at[lanes((owner * CORES + g) * group, group), :], w_buf.at[step % slots],
                w_sem.at[step % slots],
            )

    for g in range(CORES):
        for c in range(2):
            own_kv(g, c).start()
    for h in range(group):
        own_q(h).start()

    barrier = pltpu.get_barrier_semaphore()
    for offset in range(1, members):
        peer = across(member, offset, members)
        pl.semaphore_signal(barrier, inc=1, device_id=peer_id(peer), device_id_type=MESH)

    @pl.when(has_below)
    def _():
        pl.semaphore_signal(barrier, inc=1, device_id={"ctx": me - members}, device_id_type=MESH)

    @pl.when(has_above)
    def _():
        pl.semaphore_signal(barrier, inc=1, device_id={"ctx": me + members}, device_id_type=MESH)

    pl.semaphore_wait(barrier, members - 1 + has_below.astype(jnp.int32) + has_above.astype(jnp.int32))

    for g in range(CORES):
        for offset in range(1, chips):
            for c in range(2):
                give_kv(across(chip, offset, chips), g, c).start()
    for offset in range(1, members):
        for h in range(group):
            give_q(across(member, offset, members), h).start()
    if fused:
        for step in range(slots):
            load_w(step).start()

    peak[...] = jnp.full_like(peak, FLOOR)
    total[...] = jnp.zeros_like(total)
    accum[...] = jnp.zeros_like(accum)
    if fused:
        product[...] = jnp.zeros_like(product)
    gap_ref[...] = lax.broadcasted_iota(jnp.int32, (rows, block), 0) - lax.broadcasted_iota(
        jnp.int32, (rows, block), 1
    )

    def raise_own(g):
        def one(order, carry):
            up_kv(g, 0, back(chip, order, chips)).start()
            return carry

        lax.fori_loop(0, chips, one, 0)

    def from_side(g, step):
        def other(order, carry):
            at_chip = back(chip, order, chips)
            landed(kv_piece(g, plane - step, at_chip * CORES + 1 - core), kv_in.at[step, g, at_chip, 1])
            return carry

        lax.fori_loop(0, chips, other, 0)

    def take_own():
        for g in range(CORES):
            def one(order, carry):
                at_chip = back(chip, order, chips)
                piece = kv_piece(g, plane, at_chip * CORES + core)
                for c in range(2):
                    landed(piece.at[:, c * HD:(c + 1) * HD], near_in.at[g, at_chip, c])
                if g == 0:
                    @pl.when(has_above)
                    def _():
                        up_kv(g, 0, at_chip).start()

                side_kv(g, 0, at_chip).start()
                return carry

            lax.fori_loop(0, chips, one, 0)

        @pl.when(has_above & (plane == 0))
        def _():
            raise_own(1)

        for g in range(CORES):
            from_side(g, 0)

    def take(g, step):
        def one(order, carry):
            at_chip = back(chip, order, chips)
            landed(kv_piece(g, plane - step, at_chip * CORES + core), kv_in.at[step, g, at_chip, 0])

            @pl.when(has_above)
            def _():
                up_kv(g, step, at_chip).start()

            side_kv(g, step, at_chip).start()
            return carry

        lax.fori_loop(0, chips, one, 0)
        if g == 0:
            @pl.when(has_above & (step == plane))
            def _():
                raise_own(1)

        from_side(g, step)

    def chain(units):
        def score(unit):
            index, g, start, count, _ = unit
            return lax.dot_general(
                q_all[span_of(index * group + g * half, half), :], kv[pl.ds(start, count), :HD],
                (((1,), (1,)), ((), ())), preferred_element_type=jnp.float32,
            )

        pending = score(units[0])
        for n, (index, g, start, count, allow) in enumerate(units):
            following = score(units[n + 1]) if n + 1 < len(units) else None
            at = span_of(index * group + g * half, half)
            scores = jnp.concatenate(
                [jnp.where(allow(h), pending[h * rows:(h + 1) * rows], MASKED) for h in range(half)], axis=0
            )
            held = peak[at, :]
            fresh = jnp.maximum(held, jnp.max(scores, axis=-1, keepdims=True))
            peak[at, :] = fresh
            shrink = jnp.exp2((held - fresh) * scale)
            weights = jnp.exp2(scores * scale - jnp.tile(fresh * scale, (1, count // HD)))
            added = weights[:, :HD]
            for c in range(1, count // HD):
                added = added + weights[:, c * HD:(c + 1) * HD]
            total[at, :] = total[at, :] * shrink + added
            accum[at, :] = accum[at, :] * shrink + jnp.dot(
                weights.astype(jnp.bfloat16), kv[pl.ds(start, count), HD:], preferred_element_type=jnp.float32
            )
            pending = following

    def finish(g, index):
        for h in range(half):
            at = span_of(index * group + g * half + h, 1)
            mixed = accum[at, :] / jnp.sum(total[at, :], axis=-1, keepdims=True)
            done[span_of(index, 1), (g * half + h) * HD:(g * half + h + 1) * HD] = mixed.astype(jnp.bfloat16)

        @pl.when(index == member)
        def _():
            keep_o(g).start()

        @pl.when(index != member)
        def _():
            give_o(g, index).start()

    def own_tile(index):
        for h in range(group):
            landed(q_all.at[span_of(index * group + h, 1), :], q_in.at[index, h])

        def run(count):
            def allow(h):
                return gap_ref[:, :count] >= -index * rows

            chain([
                (index, g, pl.multiple_of((g * planes + plane) * block, block), count, allow) for g in range(CORES)
            ])

        short = members // 2 * rows
        if short % HD == 0 and members % 2 == 0:
            @pl.when(index < members // 2)
            def _():
                run(short)

            @pl.when(index >= members // 2)
            def _():
                run(block)
        else:
            run(block)

        @pl.when(plane == 0)
        def _():
            for g in range(CORES):
                finish(g, index)

    def far_pair(g, step, pair):
        start = pl.multiple_of((g * planes + plane - step) * block, block)

        def unit(index):
            def allow(h):
                gap = gap_ref[...]
                near = gap < windows[g * half + h] - (step * block + index * rows)
                column = lax.broadcasted_iota(jnp.int32, (rows, MOST_SINK), 1)
                sunk = near[:, :MOST_SINK] | (column < sinks[g * half + h] - (plane - step) * block)
                return jnp.concatenate([sunk, near[:, MOST_SINK:]], axis=1)

            return index, g, start, block, allow

        indices = [across(member, pair * 2 + n, members) for n in range(2)]
        chain([unit(index) for index in indices])

        @pl.when(step == plane)
        def _():
            for index in indices:
                finish(g, index)

    pairs = members // 2
    take_own()

    def first(pair, carry):
        for n in range(2):
            own_tile(across(member, pair * 2 + n, members))

        @pl.when(has_below)
        def _():
            @pl.when(pair == 0)
            def _():
                take(0, 1)

            far_pair(0, 1, pair)

        @pl.when((pair == pairs // 2) & (plane > 1))
        def _():
            take(0, 2)

        return carry

    lax.fori_loop(0, pairs, first, 0)

    def far_pairs(g, step):
        def one(order, carry):
            far_pair(g, step, pairs - 1 - order)
            return carry

        lax.fori_loop(0, pairs, one, 0)

    def project(g):
        columns = w_buf.shape[2]
        chunk = W_COLUMNS if columns % W_COLUMNS == 0 else columns

        def one(order, carry):
            step = g * chips + order
            owner = back(chip, chips - 1 - order, chips)
            for at_core in range(CORES):
                landed(feats.at[:, lanes(head_of(owner, at_core, g), half)], o_in.at[owner * CORES + at_core, g])
            load_w(step).wait()
            slot = step % slots
            features = feats[:, lanes((owner * CORES + g) * group, group)]

            def part(c, inner):
                at = pl.ds(pl.multiple_of(c * chunk, chunk), chunk)
                product[:, at] = product[:, at] + jnp.dot(
                    features, w_buf[slot, :, at], preferred_element_type=jnp.float32
                )
                return inner

            lax.fori_loop(0, columns // chunk, part, 0)

            @pl.when(step + slots < CORES * chips)
            def _():
                load_w(step + slots).start()

            return carry

        lax.fori_loop(0, chips, one, 0)

    def far_first(step, carry):
        @pl.when(step > 2)
        def _():
            take(0, step)

        far_pairs(0, step)
        return carry

    lax.fori_loop(2, plane + 1, far_first, 0)

    def far_second(step, carry):
        if fused:
            @pl.when((step == plane) & (plane == planes - 1))
            def _():
                project(0)

        take(1, step)
        far_pairs(1, step)
        return carry

    lax.fori_loop(1, plane + 1, far_second, 0)

    if fused:
        @pl.when(has_above | (plane == 0))
        def _():
            project(0)

        project(1)
        out_ref[...] = product[...].astype(out_ref.dtype)
    else:
        for g in range(CORES):
            for source in range(members):
                at = lanes(head_of(source // CORES, source % CORES, g), half)
                landed(feats.at[:, at], o_in.at[source, g])
        out_ref[...] = feats[...]

    for g in range(CORES):
        for offset in range(1, chips):
            for c in range(2):
                give_kv(across(chip, offset, chips), g, c).wait_send()
        for offset in range(1, members):
            give_o(g, across(member, offset, members)).wait_send()
    for offset in range(1, members):
        for h in range(group):
            give_q(across(member, offset, members), h).wait_send()

    def sent(step, carry):
        def one(at_chip, inner):
            for g in range(CORES):
                @pl.when(has_above)
                def _():
                    up_kv(g, step, at_chip).wait_send()

                side_kv(g, step, at_chip).wait_send()
            return inner

        return lax.fori_loop(0, chips, one, carry)

    lax.fori_loop(0, plane + 1, sent, 0)


def body(planes, members, fused, queries, keys, values, retrieval, spans, out_weight):
    rows = queries.shape[0]
    group = queries.shape[1] // keys.shape[1]
    chips, half = members // CORES, group // CORES
    block = members * rows
    if block > LEAST_RECENT or block % HD or block < MOST_SINK or group % CORES or members % CORES:
        raise ValueError("block size")
    anywhere = pl.BlockSpec(memory_space=pl.ANY)
    smem = pl.BlockSpec(memory_space=pltpu.SMEM)
    stacked = group * block
    scratch = [
        pltpu.VMEM((stacked, HD), jnp.bfloat16),
        pltpu.VMEM((CORES * planes * block, 2 * HD), jnp.bfloat16),
        pltpu.VMEM((stacked, HD), jnp.float32),
        pltpu.VMEM((stacked, HD), jnp.float32),
        pltpu.VMEM((stacked, HD), jnp.float32),
        pltpu.VMEM((block, group * HD), jnp.bfloat16),
        pltpu.VMEM((rows, members * group * HD), jnp.bfloat16),
        pltpu.VMEM((rows, block), jnp.int32),
        pltpu.SemaphoreType.DMA((CORES, chips, 2)),
        pltpu.SemaphoreType.DMA((chips, CORES, 2)),
        pltpu.SemaphoreType.DMA((planes, CORES, chips, 2)),
        pltpu.SemaphoreType.DMA((planes, CORES, chips)),
        pltpu.SemaphoreType.DMA((planes, CORES, chips)),
        pltpu.SemaphoreType.DMA((members, group)),
        pltpu.SemaphoreType.DMA((members, group)),
        pltpu.SemaphoreType.DMA((members, CORES)),
        pltpu.SemaphoreType.DMA((members, CORES)),
    ]
    operands = [queries, keys, values, retrieval, spans]
    in_specs = [anywhere, anywhere, anywhere, smem, smem]
    columns = members * group * HD
    if fused:
        columns = out_weight.shape[1]
        slots = min(W_SLOTS, members)
        operands.append(out_weight)
        in_specs.append(anywhere)
        scratch += [
            pltpu.VMEM((slots, group * HD, columns), jnp.bfloat16),
            pltpu.VMEM((rows, columns), jnp.float32),
            pltpu.SemaphoreType.DMA((slots,)),
        ]
    result = pl.pallas_call(
        functools.partial(layer_kernel, planes, members, rows, group, fused),
        out_shape=jax.ShapeDtypeStruct((rows, columns), jnp.bfloat16),
        in_specs=in_specs,
        out_specs=pl.BlockSpec(memory_space=pltpu.VMEM),
        scratch_shapes=scratch,
        compiler_params=pltpu.CompilerParams(
            collective_id=0, has_side_effects=True, vmem_limit_bytes=62 * 2 ** 20
        ),
    )(*operands)
    if fused:
        return result
    features = lax.all_gather(result, "head", axis=1, tiled=True)
    return jnp.dot(features, out_weight, preferred_element_type=jnp.float32).astype(jnp.bfloat16)


def solution(mesh):
    ctx, heads = mesh.shape["ctx"], mesh.shape["head"]

    def step(queries, keys, values, retrieval, spans, out_weight):
        members = keys.shape[1] // HD
        if ctx % members:
            raise ValueError("members")
        return body(ctx // members, members, heads == 1, queries, keys, values, retrieval, spans, out_weight)

    in_specs = (P("ctx", "head"), P("ctx", "head"), P("ctx", "head"), P(), P(), P(None, "head"))
    return jax.shard_map(step, mesh=mesh, in_specs=in_specs, out_specs=P("ctx", "head"), check_vma=False)
```

time: 118 us -> 110 us (0.932)
  Pallas kernels: 114 us -> 107 us
    pallas_call x1, Pallas kernels: 114 us -> 107 us  [body(): pl.pallas_call(functools.partial(layer_kernel, planes, members, rows, gro...]
where the time goes in v2:
time: 110 us; the launch traced here: 109 us
  Pallas kernels  107 us (97%)
  local copies, waits for them, and re-layouts  2.7 us (2%)
    pallas_call x1, Pallas kernels, body(): pl.pallas_call(functools.partial(layer_kernel, planes, members, rows, gro...  107 us
    unnamed x1, local copies, waits for them, and re-layouts  2.7 us

profile of v2, /device:TPU:29, one launch (start us, length us, event | category | flops | bytes accessed | tf_op | source)
XLA Modules:
  0.0 109.5 jit_solution(4153459595489060736)
XLA Ops:
  0.0 106.8 %shard_map.64 = bf16[192,4096]{1,0:T(8,128)(2,1)} custom-call(bf16[192,4096]{1,0:T(8,128)(2,1)} %q_hbm.1, bf16[192,1024]{1,0:T(8,128)(2,1)} %k_hbm.1, bf16[192,1024]{1,0:T(8,128)(2,1)} %v_hbm.1, s32[32]{0:T(128)} %retrieval_ref.1, s32[2,32]{1,0:T(2,128)} %spans_ref.1, bf16[4096,4096]{1,0:T(8,128)(2,1)} %rest_0_.1), custom_call_target="tpu_custom_call" | custom-call | tf_op jit(solution)/shard_map/pallas_call | solution.py:509
  106.8 2.7 %copy.8 = bf16[192,4096]{1,0:T(8,128)(2,1)} copy(bf16[192,4096]{1,0:T(8,128)(2,1)} %shard_map.64) | data formatting | bytes 3145728
